TPU v7x, 128 devices: a whole 4x4x4 slice. The times are simulated.
128 devices in a mesh: tm: 32 (over y_lo, x, z), space: 4 (over y_hi, core).
Axes of the slice: x: 4, y: 4 (y_hi: 2, y_lo: 2; y = y_hi * 2 + y_lo), z: 4, core: 2. Of those that a mesh axis runs over, the one named last changes fastest.
Arguments:
- start_block: float32 [32, 2, 3, 32, 32, 256], P('tm', None, None, None, 'space'), may hold values from -6 to 6
- gauge_links: float32 [32, 3, 2, 3, 3, 32, 256], P('tm', None, None, None, None, 'space'), may hold values from -1 to 1, as said below
- stored_vectors: bfloat16 [32, 448, 2, 3, 32, 256], P('tm', None, None, None, 'space'), may hold values from -0.02734375 to 0.02734375
Outputs:
- correlations: float32 [32, 448, 64], P('tm', 'space')
- solver_blocks: bfloat16 [32, 32, 256, 192], P('space', None, 'tm')
Inputs may be any that keep to these rules, and one draw needn't show every extreme that they name: Every link matrix gauge_links[t, mu, 0] + i gauge_links[t, mu, 1] at a site is special unitary, drawn independently at every site and direction.
All inputs are finite; a program needn't handle non-finite values.
Results may differ from a plain program's by a relative error of at most 0.0029.
Values may be sent and summed in bfloat16 or wider, within the bound.
A program may use at most 128 MiB of HBM per device.

v0:
```python
import jax
import jax.numpy as jnp
from jax import lax
from jax.experimental import pallas as pl
from jax.experimental.pallas import tpu as pltpu
from jax.sharding import PartitionSpec as P

F32 = jnp.float32
BF16 = jnp.bfloat16

NVEC = 32
LZ = 16
LAYERS = 8
HALVES = 2
LANES = 128
PC = 6
ROWS = 24
FIRST = 8
LAST = 15
BELOW = 7
ABOVE = 16
BATCHES = 8
PER_BATCH = NVEC // BATCHES
HALO_ROWS = PC * PER_BATCH * HALVES
APPLICATIONS = 4
STORE_BLOCK = 32


def lane_index():
    return lax.broadcasted_iota(jnp.int32, (LAYERS, LANES), 1)


def y_forward(low, high):
    lane = lane_index()
    a, b = pltpu.roll(low, LANES - LZ, 1), pltpu.roll(high, LANES - LZ, 1)
    keep = lane < LANES - LZ
    return jnp.where(keep, a, b), jnp.where(keep, b, a)


def y_backward(low, high):
    lane = lane_index()
    a, b = pltpu.roll(low, LZ, 1), pltpu.roll(high, LZ, 1)
    keep = lane >= LZ
    return jnp.where(keep, a, b), jnp.where(keep, b, a)


def z_forward(tile):
    along_z = lane_index() % LZ
    return jnp.where(along_z == LZ - 1, pltpu.roll(tile, LZ - 1, 1), pltpu.roll(tile, LANES - 1, 1))


def z_backward(tile):
    along_z = lane_index() % LZ
    return jnp.where(along_z == 0, pltpu.roll(tile, LANES - LZ + 1, 1), pltpu.roll(tile, 1, 1))


def kernel(
    start_ref, links_ref, stored_ref, corr_ref, solver_ref,
    x_buf, a_buf, b_buf, raw, coef, top_send, top_recv, halo_send, halo_recv,
    stored, blocks, turned, product, part_send, part_recv,
    in_sem, stored_sem, top_sem, halo_send_sem, halo_recv_sem,
    block_send_sem, block_recv_sem, own_sem, part_send_sem, part_recv_sem,
):
    me_t = lax.axis_index("tm")
    me_s = lax.axis_index("space")
    up = lax.rem(me_s + 1, 4)
    down = lax.rem(me_s + 3, 4)
    target_space = me_t // 8
    source_first = me_s * 8
    has_self = target_space == me_s

    copies_in = []
    for h in range(HALVES):
        lanes = pl.ds(h * LANES, LANES)
        copies_in.append(pltpu.make_async_copy(
            start_ref.at[:, :, :, :, lanes],
            x_buf.at[:, :, :, h, pl.ds(FIRST, LAYERS), :],
            in_sem.at[h],
        ))
        copies_in.append(pltpu.make_async_copy(
            links_ref.at[:, :, :, :, lanes],
            raw.at[:, :, :, h, pl.ds(FIRST, LAYERS), :],
            in_sem.at[2 + h],
        ))
    for copy in copies_in:
        copy.start()
    stored_copy = pltpu.make_async_copy(stored_ref, stored, stored_sem)
    stored_copy.start()

    barrier = pltpu.get_barrier_semaphore()
    for step in range(1, 4):
        pl.semaphore_signal(barrier, inc=1, device_id={"space": lax.rem(me_s + step, 4)}, device_id_type=pl.DeviceIdType.MESH)

    def greet(i, carry):
        tm_of = source_first + i // 4
        space_of = lax.rem(i, 4)

        @pl.when(jnp.logical_not(jnp.logical_and(tm_of == me_t, space_of == me_s)))
        def _():
            pl.semaphore_signal(barrier, inc=1, device_id=(tm_of, space_of), device_id_type=pl.DeviceIdType.MESH)

        return carry

    lax.fori_loop(0, 32, greet, 0)

    copies_in[1].wait()
    copies_in[3].wait()

    raw_rows = raw.reshape(54 * HALVES * ROWS, LANES)
    top_send[...] = raw_rows[pl.ds(LAST, 36, stride=ROWS), :]

    pl.semaphore_wait(barrier, 35 - has_self.astype(jnp.int32))

    top_copy = pltpu.make_async_remote_copy(
        top_send, top_recv, top_sem.at[0], top_sem.at[1],
        device_id={"space": up}, device_id_type=pl.DeviceIdType.MESH,
    )
    top_copy.start()

    def halo_copy(level, side, batch):
        return pltpu.make_async_remote_copy(
            halo_send.at[level, side, batch],
            halo_recv.at[level, side, batch],
            halo_send_sem.at[level, side, batch],
            halo_recv_sem.at[level, side, batch],
            device_id={"space": up if side else down},
            device_id_type=pl.DeviceIdType.MESH,
        )

    def flat(buf):
        return buf.reshape(PC * NVEC * HALVES * ROWS, LANES)

    def send_halo(level, buf, batch):
        rows = flat(buf)
        for side in range(2):
            row = LAST if side else FIRST
            pieces = []
            for pc in range(PC):
                base = ((pc * NVEC + batch * PER_BATCH) * HALVES) * ROWS + row
                pieces.append(rows[pl.ds(base, PER_BATCH * HALVES, stride=ROWS), :])
            halo_send[level, side, batch] = jnp.concatenate(pieces, axis=0).astype(BF16)
            halo_copy(level, side, batch).start()

    def take_halo(level, buf, batch):
        rows = flat(buf)
        for side in range(2):
            row = BELOW if side else ABOVE
            halo_copy(level, side, batch).wait_recv()
            values = halo_recv[level, side, batch].astype(F32)
            for pc in range(PC):
                base = ((pc * NVEC + batch * PER_BATCH) * HALVES) * ROWS + row
                count = PER_BATCH * HALVES
                rows[pl.ds(base, count, stride=ROWS), :] = values[pc * count:(pc + 1) * count]

    copies_in[0].wait()
    copies_in[2].wait()

    def first_halo(batch, carry):
        send_halo(0, x_buf, batch)
        return carry

    lax.fori_loop(0, BATCHES, first_halo, 0)

    def put(direction, entry, half, re, im):
        coef[direction, entry, 0, half] = re
        coef[direction, entry, 1, half] = im - re
        coef[direction, entry, 2, half] = re + im

    def centre(d, part, entry, half):
        return raw[d, part, entry, half, FIRST:FIRST + LAYERS, :]

    def prepare(entry, carry):
        mirrored = lax.rem(entry, 3) * 3 + entry // 3
        for d in range(3):
            for half in range(HALVES):
                put(2 * d, entry, half, centre(d, 0, entry, half), centre(d, 1, entry, half))
        low = y_backward(centre(1, 0, entry, 0), centre(1, 0, entry, 1))
        high = y_backward(centre(1, 1, entry, 0), centre(1, 1, entry, 1))
        for half in range(HALVES):
            put(3, mirrored, half, low[half], -high[half])
            put(5, mirrored, half, z_backward(centre(2, 0, entry, half)), -z_backward(centre(2, 1, entry, half)))
        return carry

    lax.fori_loop(0, 9, prepare, 0)

    top_copy.wait_recv()
    raw_rows[pl.ds(BELOW, 36, stride=ROWS), :] = top_recv[...]

    def prepare_below(entry, carry):
        mirrored = lax.rem(entry, 3) * 3 + entry // 3
        for half in range(HALVES):
            re = raw[0, 0, entry, half, pl.ds(BELOW, LAYERS), :]
            im = raw[0, 1, entry, half, pl.ds(BELOW, LAYERS), :]
            put(1, mirrored, half, re, -im)
        return carry

    lax.fori_loop(0, 9, prepare_below, 0)

    def hop_sums(src, v):
        sums = [[None] * 9 for _ in range(HALVES)]

        def add(direction, half, parts):
            for row in range(3):
                for col in range(3):
                    re, im = parts[col], parts[3 + col]
                    for kind, value in enumerate((parts[6 + col], re, im)):
                        term = coef[direction, row * 3 + col, kind, half] * value
                        at = row * 3 + kind
                        sums[half][at] = term if sums[half][at] is None else sums[half][at] + term

        def extended(parts):
            return parts + [parts[c] + parts[3 + c] for c in range(3)]

        own = [[src[pc // 3, pc % 3, v, half, FIRST:FIRST + LAYERS, :] for pc in range(PC)] for half in range(HALVES)]
        for half in range(HALVES):
            add(0, half, extended([src[pc // 3, pc % 3, v, half, pl.ds(FIRST + 1, LAYERS), :] for pc in range(PC)]))
            add(1, half, extended([src[pc // 3, pc % 3, v, half, pl.ds(FIRST - 1, LAYERS), :] for pc in range(PC)]))
        for direction, shift in ((2, y_forward), (3, y_backward)):
            moved = [shift(own[0][pc], own[1][pc]) for pc in range(PC)]
            for half in range(HALVES):
                add(direction, half, extended([m[half] for m in moved]))
        for direction, shift in ((4, z_forward), (5, z_backward)):
            for half in range(HALVES):
                add(direction, half, extended([shift(own[half][pc]) for pc in range(PC)]))
        out = []
        for half in range(HALVES):
            s = sums[half]
            re = [s[3 * r] - s[3 * r + 2] + 0.5 * own[half][r] for r in range(3)]
            im = [s[3 * r] + s[3 * r + 1] + 0.5 * own[half][3 + r] for r in range(3)]
            out.append(re + im)
        return out

    def apply(level, src, dst):
        def one(v, carry):
            out = hop_sums(src, v)
            for half in range(HALVES):
                for pc in range(PC):
                    value = out[half][pc]
                    at = (pc // 3, pc % 3, v, half, slice(FIRST, FIRST + LAYERS), slice(None))
                    if level == 1:
                        value = value - 36.0 * x_buf[at]
                    if level == 3:
                        value = value * (1.0 / 162.0) + x_buf[at]
                    dst[at] = value
            return carry

        def batch_step(batch, carry):
            take_halo(level, src, batch)
            lax.fori_loop(batch * PER_BATCH, (batch + 1) * PER_BATCH, one, 0)
            if level + 1 < APPLICATIONS:
                send_halo(level + 1, dst, batch)
            return carry

        lax.fori_loop(0, BATCHES, batch_step, 0)

    apply(0, x_buf, a_buf)
    apply(1, a_buf, b_buf)
    apply(2, b_buf, a_buf)
    apply(3, a_buf, b_buf)

    result_rows = flat(b_buf)

    def arrange(layer, carry):
        for half in range(HALVES):
            lanes = slice(half * LANES, (half + 1) * LANES)
            pieces = []
            for pc in range(PC):
                base = (pc * NVEC * HALVES + half) * ROWS + FIRST + layer
                pieces.append(rows_of(base))
            whole = jnp.concatenate(pieces, axis=0)
            sites = whole.T.astype(BF16)
            blocks[half * 16:(half + 1) * 16, layer] = sites.reshape(16, 8, PC * NVEC)
            for c in range(3):
                re, im = pieces[c].astype(BF16), pieces[3 + c].astype(BF16)
                at = pl.ds(pl.multiple_of(layer * 64, 64), 64)
                turned[at, c * 256 + half * LANES:c * 256 + (half + 1) * LANES] = jnp.concatenate([re, im], axis=0)
                turned[at, (3 + c) * 256 + half * LANES:(3 + c) * 256 + (half + 1) * LANES] = jnp.concatenate([im, -re], axis=0)
        return carry

    def rows_of(base):
        return result_rows[pl.ds(base, NVEC, stride=HALVES * ROWS), :]

    lax.fori_loop(0, LAYERS, arrange, 0)

    target_rows = pl.ds(me_s * LAYERS, LAYERS)
    local_t = lax.rem(me_t, 8)

    def block_copy(tm_of):
        return pltpu.make_async_remote_copy(
            blocks.at[tm_of],
            solver_ref.at[local_t, target_rows],
            block_send_sem.at[tm_of],
            block_recv_sem.at[local_t * 4 + me_s],
            device_id=(tm_of, target_space),
            device_id_type=pl.DeviceIdType.MESH,
        )

    own_copy = pltpu.make_async_copy(blocks.at[me_t], solver_ref.at[local_t, target_rows], own_sem)

    @pl.when(has_self)
    def _():
        own_copy.start()

    def send_block(i, carry):
        tm_of = lax.rem(me_t + i, 32)

        @pl.when(jnp.logical_or(i > 0, jnp.logical_not(has_self)))
        def _():
            block_copy(tm_of).start()

        return carry

    lax.fori_loop(0, 32, send_block, 0)

    stored_copy.wait()

    def correlate(block, carry):
        first = pl.multiple_of(block * STORE_BLOCK, STORE_BLOCK)
        some = [stored[pl.ds(first, STORE_BLOCK), rc].reshape(STORE_BLOCK * LAYERS, 256) for rc in range(PC)]
        left = jnp.concatenate(some, axis=1)
        product[...] = lax.dot_general(
            left, turned[...], (((1,), (1,)), ((), ())), preferred_element_type=F32
        )
        layer = lax.broadcasted_iota(jnp.int32, (STORE_BLOCK * LAYERS, LANES), 0) % LAYERS
        upper = lax.broadcasted_iota(jnp.int32, (STORE_BLOCK * LAYERS, LANES), 1) // 64
        total = jnp.zeros((STORE_BLOCK * LAYERS, LANES), F32)
        for pair in range(4):
            total = jnp.where(layer == 2 * pair + upper, product[:, pair * LANES:(pair + 1) * LANES], total)
        summed = jnp.sum(total.reshape(STORE_BLOCK, LAYERS, LANES), axis=1)
        part_send[pl.ds(first, STORE_BLOCK), :] = summed
        return carry

    lax.fori_loop(0, 448 // STORE_BLOCK, correlate, 0)

    def part_copy(step):
        other = lax.rem(me_s + step, 4)
        return pltpu.make_async_remote_copy(
            part_send.at[pl.ds(pl.multiple_of(other * 112, 8), 112)],
            part_recv.at[step - 1],
            part_send_sem.at[step - 1],
            part_recv_sem.at[step - 1],
            device_id={"space": other},
            device_id_type=pl.DeviceIdType.MESH,
        )

    for step in range(1, 4):
        part_copy(step).start()
    total = part_send[pl.ds(pl.multiple_of(me_s * 112, 8), 112), :]
    for step in range(1, 4):
        part_copy(step).wait_recv()
        total = total + part_recv[step - 1]
    folded = total[:, :64] + total[:, 64:]
    corr_ref[...] = folded.T

    def finish_halo(i, carry):
        for level in range(APPLICATIONS):
            for side in range(2):
                halo_copy(level, side, i).wait_send()
        return carry

    lax.fori_loop(0, BATCHES, finish_halo, 0)
    top_copy.wait_send()
    for step in range(1, 4):
        part_copy(step).wait_send()

    @pl.when(has_self)
    def _():
        own_copy.wait()

    def finish_block(i, carry):
        tm_of = lax.rem(me_t + i, 32)

        @pl.when(jnp.logical_or(i > 0, jnp.logical_not(has_self)))
        def _():
            block_copy(tm_of).wait_send()

        return carry

    lax.fori_loop(0, 32, finish_block, 0)

    def take_block(i, carry):
        tm_of = source_first + i // 4
        space_of = lax.rem(i, 4)

        @pl.when(jnp.logical_not(jnp.logical_and(tm_of == me_t, space_of == me_s)))
        def _():
            pltpu.make_async_remote_copy(
                blocks.at[0],
                solver_ref.at[i // 4, pl.ds(space_of * LAYERS, LAYERS)],
                block_send_sem.at[0],
                block_recv_sem.at[i],
                device_id=(tm_of, space_of),
                device_id_type=pl.DeviceIdType.MESH,
            ).wait_recv()

        return carry

    lax.fori_loop(0, 32, take_block, 0)


def shards(start_block, gauge_links, stored_vectors):
    any_space = pl.BlockSpec(memory_space=pl.ANY)
    buffer = pltpu.VMEM((2, 3, NVEC, HALVES, ROWS, LANES), F32)
    halo = pltpu.VMEM((APPLICATIONS, 2, BATCHES, HALO_ROWS, LANES), BF16)
    halo_sem = pltpu.SemaphoreType.DMA((APPLICATIONS, 2, BATCHES))
    corr, solver = pl.pallas_call(
        kernel,
        out_shape=(
            jax.ShapeDtypeStruct((64, 112), F32),
            jax.ShapeDtypeStruct((8, 32, 8, 192), BF16),
        ),
        in_specs=[any_space] * 3,
        out_specs=(pl.BlockSpec(memory_space=pltpu.VMEM), any_space),
        scratch_shapes=[
            buffer, buffer, buffer,
            pltpu.VMEM((3, 2, 9, HALVES, ROWS, LANES), F32),
            pltpu.VMEM((6, 9, 3, HALVES, LAYERS, LANES), F32),
            pltpu.VMEM((36, LANES), F32),
            pltpu.VMEM((36, LANES), F32),
            halo, halo,
            pltpu.VMEM((448, 6, LAYERS, 256), BF16),
            pltpu.VMEM((32, LAYERS, 8, 192), BF16),
            pltpu.VMEM((512, 1536), BF16),
            pltpu.VMEM((STORE_BLOCK * LAYERS, 512), F32),
            pltpu.VMEM((448, LANES), F32),
            pltpu.VMEM((3, 112, LANES), F32),
            pltpu.SemaphoreType.DMA((4,)),
            pltpu.SemaphoreType.DMA,
            pltpu.SemaphoreType.DMA((2,)),
            halo_sem, halo_sem,
            pltpu.SemaphoreType.DMA((32,)),
            pltpu.SemaphoreType.DMA((32,)),
            pltpu.SemaphoreType.DMA,
            pltpu.SemaphoreType.DMA((3,)),
            pltpu.SemaphoreType.DMA((3,)),
        ],
        compiler_params=pltpu.CompilerParams(
            collective_id=0, has_side_effects=True, vmem_limit_bytes=60 * 1024 * 1024
        ),
    )(
        start_block[0],
        gauge_links[0].reshape(3, 2, 9, LAYERS, 256),
        stored_vectors[0].reshape(448, 6, LAYERS, 256),
    )
    return corr.T[None], solver


def solution(mesh):
    in_specs = (
        P("tm", None, None, None, "space", None),
        P("tm", None, None, None, None, "space", None),
        P("tm", None, None, None, "space", None),
    )
    out_specs = (P("tm", "space", None), P("space", None, "tm", None))
    return jax.shard_map(shards, mesh=mesh, in_specs=in_specs, out_specs=out_specs, check_vma=False)
```

profile of v0, /device:TPU:1, one launch (start us, length us, event | category | flops | bytes accessed | tf_op | source)
XLA Modules:
  0.0 62.5 jit_solution(10071353121857006378)
XLA Ops:
  0.6 58.3 %shard_map.50 = (f32[64,112]{1,0:T(8,128)}, bf16[8,32,8,192]{3,2,1,0:T(8,128)(2,1)}) custom-call(f32[2,3,32,8,256]{4,3,2,1,0:T(8,128)} %bitcast.7, f32[3,2,9,8,256]{4,3,2,1,0:T(8,128)} %bitcast.8, bf16[448,6,8,256]{3,2,1,0:T(8,128)(2,1)} %bitcast.6), custom_call_target="tpu_custom_call" | custom-call | tf_op jit(solution)/shard_map/pallas_call | solution.py:406
  58.9 1.4 %copy.7 = f32[1,112,64]{1,2,0:T(8,128)} copy(f32[1,112,64]{1,2,0:T(8,128)} %bitcast.9) | data formatting | bytes 57344
  60.3 2.3 %copy.8 = bf16[8,32,8,192]{3,2,1,0:T(8,128)(2,1)} copy(bf16[8,32,8,192]{3,2,1,0:T(8,128)(2,1)} %get-tuple-element.9) | data formatting | bytes 1572864
where the time goes:
time: 62.7 us; the launch traced here: 62.5 us
  Pallas kernels  58.3 us (93%)
  local copies, waits for them, and re-layouts  3.64 us (6%)
  between operations  0.64 us (1%)
    pallas_call x1, Pallas kernels, shards(): pl.pallas_call(kernel, out_shape=(jax.ShapeDtypeStruct((64, 112), F32), j...  58.3 us
    unnamed x2, local copies, waits for them, and re-layouts  3.64 us

commit v1 on v0

v1 whole, which is shorter than its diff:
```python
import jax
import jax.numpy as jnp
from jax import lax
from jax.experimental import pallas as pl
from jax.experimental.pallas import tpu as pltpu
from jax.sharding import PartitionSpec as P

F32 = jnp.float32
BF16 = jnp.bfloat16

NVEC = 32
LZ = 16
LAYERS = 8
HALVES = 2
LANES = 128
PC = 6
ROWS = 24
FIRST = 8
LAST = 15
BELOW = 7
ABOVE = 16
BATCHES = 8
PER_BATCH = NVEC // BATCHES
HALO_ROWS = PC * PER_BATCH * HALVES
APPLICATIONS = 4
STORE_BLOCK = 32
EARLY_BATCHES = 2
LEADS = (0, 0, 3, 6)
UNROLL = 2


def lane_index():
    return lax.broadcasted_iota(jnp.int32, (LAYERS, LANES), 1)


def y_forward(own, other):
    keep = lane_index() < LANES - LZ
    return jnp.where(keep, pltpu.roll(own, LANES - LZ, 1), pltpu.roll(other, LANES - LZ, 1))


def y_backward(own, other):
    keep = lane_index() >= LZ
    return jnp.where(keep, pltpu.roll(own, LZ, 1), pltpu.roll(other, LZ, 1))


def z_forward(tile):
    along_z = lane_index() % LZ
    return jnp.where(along_z == LZ - 1, pltpu.roll(tile, LZ - 1, 1), pltpu.roll(tile, LANES - 1, 1))


def z_backward(tile):
    along_z = lane_index() % LZ
    return jnp.where(along_z == 0, pltpu.roll(tile, LANES - LZ + 1, 1), pltpu.roll(tile, 1, 1))


def kernel(
    start_ref, links_ref, stored_ref, corr_ref, got_ref,
    x_buf, a_buf, b_buf, raw, coef, edge, top_send, top_recv, halo_send, halo_recv,
    stored, blocks, turned, product, diagonal, ones, delta, part_send, part_recv,
    in_sem, stored_sem, top_sem, halo_send_sem, halo_recv_sem,
    block_send_sem, block_recv_sem, own_sem, part_send_sem, part_recv_sem, met_sem,
):
    me_t = lax.axis_index("tm")
    me_s = lax.axis_index("space")
    up = lax.rem(me_s + 1, 4)
    down = lax.rem(me_s + 3, 4)
    target_space = me_t // 8
    source_first = me_s * 8
    has_self = target_space == me_s

    copies_in = []
    for h in range(HALVES):
        lanes = pl.ds(h * LANES, LANES)
        copies_in.append(pltpu.make_async_copy(
            start_ref.at[:, :, :, :, lanes],
            x_buf.at[:, :, :, h, pl.ds(FIRST, LAYERS), :],
            in_sem.at[h],
        ))
        copies_in.append(pltpu.make_async_copy(
            links_ref.at[:, :, :, :, lanes],
            raw.at[:, :, :, h, pl.ds(FIRST, LAYERS), :],
            in_sem.at[2 + h],
        ))
    for copy in copies_in:
        copy.start()
    stored_copy = pltpu.make_async_copy(stored_ref, stored, stored_sem)
    stored_copy.start()

    y_lo, x_at, z_at = me_t // 16, lax.rem(me_t // 4, 4), lax.rem(me_t, 4)

    def x_partner(step):
        return (y_lo * 16 + lax.rem(x_at + step, 4) * 4 + z_at, me_s)

    def z_partner(step):
        return (y_lo * 16 + x_at * 4 + lax.rem(z_at + step, 4), me_s)

    def y_partner(step):
        return (lax.rem(y_lo + step // 4, 2) * 16 + x_at * 4 + z_at, lax.rem(me_s + step, 4))

    rings = ([x_partner(i) for i in range(1, 4)], [z_partner(i) for i in range(1, 4)], [y_partner(i) for i in range(1, 8)])

    def tell(sem, ring):
        for partner in ring:
            pl.semaphore_signal(sem, inc=1, device_id=partner, device_id_type=pl.DeviceIdType.MESH)

    barrier = pltpu.get_barrier_semaphore()
    for ring in rings:
        tell(barrier, ring)

    def flat(buf):
        return buf.reshape(PC * NVEC * HALVES * ROWS, LANES)

    raw_rows = raw.reshape(54 * HALVES * ROWS, LANES)
    zeros = jnp.zeros((LAYERS, LANES), F32)

    def clear(i, carry):
        for buf in (x_buf, a_buf, b_buf):
            for row in (BELOW, ABOVE):
                flat(buf)[pl.ds(i * LAYERS * ROWS + row, LAYERS, stride=ROWS), :] = zeros
        return carry

    lax.fori_loop(0, PC * NVEC * HALVES // LAYERS, clear, 0)
    group = lax.broadcasted_iota(jnp.int32, (896, LANES), 0) // LAYERS
    ones[...] = jnp.where(group == lax.broadcasted_iota(jnp.int32, (896, LANES), 1), 1.0, 0.0).astype(BF16)
    for i in range(5):
        raw_rows[pl.ds(min(i * LAYERS, 28) * ROWS + BELOW, LAYERS, stride=ROWS), :] = zeros

    copies_in[1].wait()
    copies_in[3].wait()

    top_send[...] = raw_rows[pl.ds(LAST, 36, stride=ROWS), :]

    top_copy = pltpu.make_async_remote_copy(
        top_send, top_recv, top_sem.at[0], top_sem.at[1],
        device_id={"space": up}, device_id_type=pl.DeviceIdType.MESH,
    )

    def halo_copy(level, side, batch):
        return pltpu.make_async_remote_copy(
            halo_send.at[level, side, batch],
            halo_recv.at[level, side, batch],
            halo_send_sem.at[level, side, batch],
            halo_recv_sem.at[level, side, batch],
            device_id={"space": up if side else down},
            device_id_type=pl.DeviceIdType.MESH,
        )

    def send_halo(level, buf, batch):
        rows = flat(buf)
        for side in range(2):
            row = LAST if side else FIRST
            pieces = []
            for pc in range(PC):
                base = ((pc * NVEC + batch * PER_BATCH) * HALVES) * ROWS + row
                pieces.append(rows[pl.ds(base, PER_BATCH * HALVES, stride=ROWS), :])
            halo_send[level, side, batch] = jnp.concatenate(pieces, axis=0).astype(BF16)
            halo_copy(level, side, batch).start()

    def put(direction, entry, half, re, im):
        coef[direction, entry, 0, half] = re
        coef[direction, entry, 1, half] = im - re
        coef[direction, entry, 2, half] = re + im

    def centre(d, part, entry, half):
        return raw[d, part, entry, half, FIRST:FIRST + LAYERS, :]

    def prepare(entry, carry):
        mirrored = lax.rem(entry, 3) * 3 + entry // 3
        for d in range(3):
            for half in range(HALVES):
                put(2 * d, entry, half, centre(d, 0, entry, half), centre(d, 1, entry, half))
        for half in range(HALVES):
            re, im = [y_backward(centre(1, part, entry, half), centre(1, part, entry, 1 - half)) for part in range(2)]
            put(3, mirrored, half, re, -im)
            put(5, mirrored, half, z_backward(centre(2, 0, entry, half)), -z_backward(centre(2, 1, entry, half)))
        return carry

    lax.fori_loop(0, 9, prepare, 0)

    def prepare_below(entry, carry):
        mirrored = lax.rem(entry, 3) * 3 + entry // 3
        for half in range(HALVES):
            re = raw[0, 0, entry, half, pl.ds(BELOW, LAYERS), :]
            im = raw[0, 1, entry, half, pl.ds(BELOW, LAYERS), :]
            put(1, mirrored, half, re, -im)
        return carry

    lax.fori_loop(0, 9, prepare_below, 0)

    edge_rows = coef.reshape(6 * 9 * 3 * HALVES * LAYERS, LANES)
    half_of = lax.broadcasted_iota(jnp.int32, (LAYERS, LANES), 0) % HALVES

    def alternate(rows, first, step):
        low = jnp.broadcast_to(rows[pl.ds(first, 1), :], (LAYERS, LANES))
        high = jnp.broadcast_to(rows[pl.ds(first + step, 1), :], (LAYERS, LANES))
        return jnp.where(half_of == 0, low, high)

    def prepare_above_edge(entry, carry):
        for kind in range(3):
            edge[0, entry, kind] = alternate(edge_rows, (entry * 3 + kind) * HALVES * LAYERS + LAYERS - 1, LAYERS)
        return carry

    lax.fori_loop(0, 9, prepare_above_edge, 0)

    def prepare_below_edge(entry, carry):
        mirrored = lax.rem(entry, 3) * 3 + entry // 3
        re = alternate(top_recv, entry * HALVES, 1)
        im = -alternate(top_recv, (9 + entry) * HALVES, 1)
        edge[1, mirrored, 0] = re
        edge[1, mirrored, 1] = im - re
        edge[1, mirrored, 2] = re + im
        return carry

    def correct(level, buf, batch):
        for side in range(2):
            halo_copy(level, side, batch).wait_recv()
            row = FIRST if side else LAST
            values = halo_recv[level, side, batch].astype(F32)
            count = PER_BATCH * HALVES
            parts = [values[pc * count:(pc + 1) * count] for pc in range(PC)]
            both = [parts[c] + parts[3 + c] for c in range(3)]
            for r in range(3):
                s = [None] * 3
                for c in range(3):
                    for kind, value in enumerate((both[c], parts[c], parts[3 + c])):
                        term = edge[side, r * 3 + c, kind] * value
                        s[kind] = term if s[kind] is None else s[kind] + term
                for pc, change in ((r, s[0] - s[2]), (3 + r, s[0] + s[1])):
                    if level == 3:
                        delta[side, pc, pl.ds(pl.multiple_of(batch * count, count), count), :] = change * (1.0 / 162.0)
                    else:
                        rows = flat(buf)
                        at = pl.ds(((pc * NVEC + batch * PER_BATCH) * HALVES) * ROWS + row, count, stride=ROWS)
                        rows[at, :] = rows[at, :] + change

    def hop_sums(src, vectors, half):
        sums = [[None] * 9 for _ in vectors]

        def add(direction, parts_of):
            for row in range(3):
                for col in range(3):
                    for kind in range(3):
                        factor = coef[direction, row * 3 + col, kind, half]
                        at = row * 3 + kind
                        for i, parts in enumerate(parts_of):
                            term = factor * parts[((6, 0, 3)[kind]) + col]
                            sums[i][at] = term if sums[i][at] is None else sums[i][at] + term

        def extended(parts):
            return parts + [parts[c] + parts[3 + c] for c in range(3)]

        def tiles(v, half_of, first):
            return [src[pc // 3, pc % 3, v, half_of, pl.ds(first, LAYERS), :] for pc in range(PC)]

        own = [tiles(v, half, FIRST) for v in vectors]
        other = [tiles(v, 1 - half, FIRST) for v in vectors]
        add(0, [extended(tiles(v, half, FIRST + 1)) for v in vectors])
        add(1, [extended(tiles(v, half, FIRST - 1)) for v in vectors])
        for direction, shift in ((2, y_forward), (3, y_backward)):
            add(direction, [extended([shift(a, b) for a, b in zip(mine, theirs)]) for mine, theirs in zip(own, other)])
        for direction, shift in ((4, z_forward), (5, z_backward)):
            add(direction, [extended([shift(a) for a in mine]) for mine in own])
        out = []
        for s, mine in zip(sums, own):
            re = [s[3 * r] - s[3 * r + 2] + 0.5 * mine[r] for r in range(3)]
            im = [s[3 * r] + s[3 * r + 1] + 0.5 * mine[3 + r] for r in range(3)]
            out.append(re + im)
        return out

    def apply_pair(level, src, dst, v, half):
        vectors = [v, v + 1]
        for at_v, out in zip(vectors, hop_sums(src, vectors, half)):
            for pc in range(PC):
                value = out[pc]
                at = (pc // 3, pc % 3, at_v, half, pl.ds(FIRST, LAYERS), slice(None))
                if level == 1:
                    value = value - 36.0 * x_buf[at]
                if level == 3:
                    value = value * (1.0 / 162.0) + x_buf[at]
                dst[at] = value

    def correct_source(level, src, batch):
        correct(level - 1, src, batch)
        send_halo(level, src, batch)

    def correct_ahead(level, src, batch):
        ahead = batch + LEADS[level]

        @pl.when(ahead < BATCHES)
        def _():
            correct_source(level, src, ahead)

    def correct_first(level, src):
        def step(batch, carry):
            correct_source(level, src, batch)
            return carry

        lax.fori_loop(0, LEADS[level], step, 0)

    def batches(level, src, dst, first, last):
        def step(batch, carry):
            if level:
                correct_ahead(level, src, batch)

            def pair(i, inner):
                apply_pair(level, src, dst, batch * PER_BATCH + 2 * (i // HALVES), lax.rem(i, HALVES))
                return inner

            lax.fori_loop(0, PER_BATCH, pair, 0, unroll=UNROLL)
            return carry

        lax.fori_loop(first, last, step, 0)

    def first_halo(batch, carry):
        send_halo(0, x_buf, batch)
        return carry

    copies_in[0].wait()
    copies_in[2].wait()
    batches(0, x_buf, a_buf, 0, EARLY_BATCHES)
    pl.semaphore_wait(barrier, sum(len(ring) for ring in rings))
    top_copy.start()
    lax.fori_loop(0, BATCHES, first_halo, 0)
    tell(met_sem.at[0], rings[0])
    batches(0, x_buf, a_buf, EARLY_BATCHES, BATCHES)
    top_copy.wait_recv()
    lax.fori_loop(0, 9, prepare_below_edge, 0)
    pl.semaphore_wait(met_sem.at[0], len(rings[0]))
    tell(met_sem.at[1], rings[1])
    batches(1, a_buf, b_buf, 0, BATCHES)
    pl.semaphore_wait(met_sem.at[1], len(rings[1]))
    tell(met_sem.at[2], rings[2])
    correct_first(2, b_buf)
    batches(2, b_buf, a_buf, 0, BATCHES)
    correct_first(3, a_buf)

    result_rows = flat(b_buf)
    local_t = lax.rem(me_t, 8)

    def block_copy(tm_of):
        return pltpu.make_async_remote_copy(
            blocks.at[tm_of],
            got_ref.at[local_t, me_s],
            block_send_sem.at[tm_of],
            block_recv_sem.at[local_t * 4 + me_s],
            device_id=(tm_of, target_space),
            device_id_type=pl.DeviceIdType.MESH,
        )

    own_copy = pltpu.make_async_copy(blocks.at[me_t], got_ref.at[local_t, me_s], own_sem)

    def destination(half, i):
        return half * 16 + lax.rem(x_at + i // 4, 4) * 4 + lax.rem(z_at + i, 4)

    def foreign(tm_of):
        return jnp.logical_not(jnp.logical_and(has_self, tm_of == me_t))

    def last_half(half):
        def step(batch, carry):
            if half == 0:
                correct_ahead(3, a_buf, batch)

            def pair(i, inner):
                apply_pair(3, a_buf, b_buf, batch * PER_BATCH + 2 * i, half)
                return inner

            lax.fori_loop(0, PER_BATCH // 2, pair, 0, unroll=UNROLL)
            return carry

        lax.fori_loop(0, BATCHES, step, 0)

        if half == 0:
            def last_corrections(batch, carry):
                correct(3, None, batch)
                return carry

            lax.fori_loop(0, BATCHES, last_corrections, 0)

        for side in range(2):
            row = FIRST if side else LAST
            for pc in range(PC):
                at = pl.ds((pc * NVEC * HALVES + half) * ROWS + row, NVEC, stride=HALVES * ROWS)
                result_rows[at, :] = result_rows[at, :] + delta[side, pc, pl.ds(half, NVEC, stride=HALVES), :]

        def arrange(layer, carry):
            tiles = []
            for x in (layer, layer + 4):
                pieces = []
                for pc in range(PC):
                    base = (pc * NVEC * HALVES + half) * ROWS + FIRST + x
                    pieces.append(result_rows[pl.ds(base, NVEC, stride=HALVES * ROWS), :])
                tiles.append(pieces)
                blocks[half * 16:(half + 1) * 16, x] = jnp.concatenate(pieces[:4], axis=0).T.astype(BF16).reshape(16, 8, LANES)
                for c in range(3):
                    re, im = pieces[c].astype(BF16), pieces[3 + c].astype(BF16)
                    at = pl.ds(pl.multiple_of(x * 64, 64), 64)
                    first = c * 256 + half * LANES
                    turned[at, first:first + LANES] = jnp.concatenate([re, im], axis=0)
                    turned[at, 768 + first:768 + first + LANES] = jnp.concatenate([im, -re], axis=0)
            rest = jnp.concatenate(tiles[0][4:] + tiles[1][4:], axis=0)
            blocks[half * 16:(half + 1) * 16, 8 + layer] = rest.T.astype(BF16).reshape(16, 8, LANES)
            return carry

        lax.fori_loop(0, 4, arrange, 0)

        if half == 0:
            pl.semaphore_wait(met_sem.at[2], len(rings[2]))

        def send_block(i, carry):
            tm_of = destination(half, i)

            @pl.when(foreign(tm_of))
            def _():
                block_copy(tm_of).start()

            return carry

        lax.fori_loop(0, 16, send_block, 0)

    last_half(0)
    last_half(1)

    @pl.when(has_self)
    def _():
        own_copy.start()

    stored_copy.wait()

    def correlate(block, carry):
        first = pl.multiple_of(block * STORE_BLOCK, STORE_BLOCK)
        some = [stored[pl.ds(first, STORE_BLOCK), rc].reshape(STORE_BLOCK * LAYERS, 256) for rc in range(PC)]
        product[...] = lax.dot_general(
            turned[...], jnp.concatenate(some, axis=1), (((1,), (1,)), ((), ())), preferred_element_type=F32
        )
        layer = lax.broadcasted_iota(jnp.int32, (64, STORE_BLOCK * LAYERS), 1) % LAYERS
        total = product[0:64]
        for x in range(1, LAYERS):
            total = jnp.where(layer == x, product[x * 64:(x + 1) * 64], total)
        diagonal[:, pl.ds(pl.multiple_of(block * 256, 256), 256)] = total
        return carry

    lax.fori_loop(0, 448 // STORE_BLOCK, correlate, 0)

    def part_copy(step):
        other = lax.rem(me_s + step, 4)
        return pltpu.make_async_remote_copy(
            part_send.at[other],
            part_recv.at[step - 1],
            part_send_sem.at[step - 1],
            part_recv_sem.at[step - 1],
            device_id={"space": other},
            device_id_type=pl.DeviceIdType.MESH,
        )

    for owner in range(4):
        values = diagonal[:, owner * 896:(owner + 1) * 896]
        high = values.astype(BF16)
        low = (values - high.astype(F32)).astype(BF16)
        both = jnp.dot(jnp.concatenate([high, low], axis=0), ones[...], preferred_element_type=F32)
        part_send[owner] = both[:64] + both[64:]
    for step in range(1, 4):
        part_copy(step).start()
    total = part_send[me_s]
    for step in range(1, 4):
        part_copy(step).wait_recv()
        total = total + part_recv[step - 1]
    corr_ref[...] = total[:, :112]

    def finish_halo(i, carry):
        for level in range(APPLICATIONS):
            for side in range(2):
                halo_copy(level, side, i).wait_send()
        return carry

    lax.fori_loop(0, BATCHES, finish_halo, 0)
    top_copy.wait_send()
    for step in range(1, 4):
        part_copy(step).wait_send()

    @pl.when(has_self)
    def _():
        own_copy.wait()

    def finish_block(i, carry):
        for half in range(HALVES):
            tm_of = destination(half, i)

            @pl.when(foreign(tm_of))
            def _():
                block_copy(tm_of).wait_send()

        return carry

    lax.fori_loop(0, 16, finish_block, 0)

    def take_block(i, carry):
        tm_of = source_first + i // 4
        space_of = lax.rem(i, 4)

        @pl.when(jnp.logical_not(jnp.logical_and(tm_of == me_t, space_of == me_s)))
        def _():
            pltpu.make_async_remote_copy(
                blocks.at[0],
                got_ref.at[i // 4, space_of],
                block_send_sem.at[0],
                block_recv_sem.at[i],
                device_id=(tm_of, space_of),
                device_id_type=pl.DeviceIdType.MESH,
            ).wait_recv()

        return carry

    lax.fori_loop(0, 32, take_block, 0)


def unpack(corr_ref, got_ref, corr_out, solver_out):
    corr_out[...] = corr_ref[...]
    for t in range(2):
        for s in range(4):
            solver_out[t, s * 8:(s + 1) * 8, :, :LANES] = got_ref[t, s, 0:8]
            rest = got_ref[t, s, 8:12]
            solver_out[t, s * 8:s * 8 + 4, :, LANES:] = rest[:, :, :64]
            solver_out[t, s * 8 + 4:s * 8 + 8, :, LANES:] = rest[:, :, 64:]


def shards(start_block, gauge_links, stored_vectors):
    any_space = pl.BlockSpec(memory_space=pl.ANY)
    buffer = pltpu.VMEM((2, 3, NVEC, HALVES, ROWS, LANES), F32)
    halo = pltpu.VMEM((APPLICATIONS, 2, BATCHES, HALO_ROWS, LANES), BF16)
    halo_sem = pltpu.SemaphoreType.DMA((APPLICATIONS, 2, BATCHES))
    corr, got = pl.pallas_call(
        kernel,
        out_shape=(
            jax.ShapeDtypeStruct((64, 112), F32),
            jax.ShapeDtypeStruct((8, 4, 12, 8, LANES), BF16),
        ),
        in_specs=[any_space] * 3,
        out_specs=(pl.BlockSpec(memory_space=pltpu.VMEM), any_space),
        scratch_shapes=[
            buffer, buffer, buffer,
            pltpu.VMEM((3, 2, 9, HALVES, ROWS, LANES), F32),
            pltpu.VMEM((6, 9, 3, HALVES, LAYERS, LANES), F32),
            pltpu.VMEM((2, 9, 3, LAYERS, LANES), F32),
            pltpu.VMEM((36, LANES), F32),
            pltpu.VMEM((36, LANES), F32),
            halo, halo,
            pltpu.VMEM((448, 6, LAYERS, 256), BF16),
            pltpu.VMEM((32, 12, 8, LANES), BF16),
            pltpu.VMEM((512, 1536), BF16),
            pltpu.VMEM((512, STORE_BLOCK * LAYERS), F32),
            pltpu.VMEM((64, 448 * LAYERS), F32),
            pltpu.VMEM((896, LANES), BF16),
            pltpu.VMEM((2, PC, NVEC * HALVES, LANES), F32),
            pltpu.VMEM((4, 64, LANES), F32),
            pltpu.VMEM((3, 64, LANES), F32),
            pltpu.SemaphoreType.DMA((4,)),
            pltpu.SemaphoreType.DMA,
            pltpu.SemaphoreType.DMA((2,)),
            halo_sem, halo_sem,
            pltpu.SemaphoreType.DMA((32,)),
            pltpu.SemaphoreType.DMA((32,)),
            pltpu.SemaphoreType.DMA,
            pltpu.SemaphoreType.DMA((3,)),
            pltpu.SemaphoreType.DMA((3,)),
            pltpu.SemaphoreType.REGULAR((3,)),
        ],
        compiler_params=pltpu.CompilerParams(
            collective_id=0, has_side_effects=True, vmem_limit_bytes=60 * 1024 * 1024
        ),
    )(
        start_block[0],
        gauge_links[0].reshape(3, 2, 9, LAYERS, 256),
        stored_vectors[0].reshape(448, 6, LAYERS, 256),
    )
    corr, solver = pl.pallas_call(
        unpack,
        grid=(4,),
        out_shape=(
            jax.ShapeDtypeStruct((64, 112), F32),
            jax.ShapeDtypeStruct((8, 32, 8, 192), BF16),
        ),
        in_specs=[
            pl.BlockSpec((64, 112), lambda i: (0, 0)),
            pl.BlockSpec((2, 4, 12, 8, LANES), lambda i: (i, 0, 0, 0, 0)),
        ],
        out_specs=(
            pl.BlockSpec((64, 112), lambda i: (0, 0)),
            pl.BlockSpec((2, 32, 8, 192), lambda i: (i, 0, 0, 0)),
        ),
    )(corr, got)
    return corr.T[None], solver


def solution(mesh):
    in_specs = (
        P("tm", None, None, None, "space", None),
        P("tm", None, None, None, None, "space", None),
        P("tm", None, None, None, "space", None),
    )
    out_specs = (P("tm", "space", None), P("space", None, "tm", None))
    return jax.shard_map(shards, mesh=mesh, in_specs=in_specs, out_specs=out_specs, check_vma=False)
```

time: 62.7 us -> 51.1 us (0.81)
  the two profiles are of different devices: /device:TPU:1 before, /device:TPU:25 now
where the time goes in v1:
time: 51.1 us; the launch traced here: 51 us
  Pallas kernels  50.3 us (98%)
  between operations  0.64 us (1%)
    pallas_call x1, Pallas kernels, shards(): pl.pallas_call(kernel, out_shape=(jax.ShapeDtypeStruct((64, 112), F32), j...  46.8 us
    pallas_call x1, Pallas kernels, shards(): pl.pallas_call(unpack, grid=(4,), out_shape=(jax.ShapeDtypeStruct((64, 11...  3.49 us

profile of v1, /device:TPU:25, one launch (start us, length us, event | category | flops | bytes accessed | tf_op | source)
XLA Modules:
  0.0 51.0 jit_solution(17328124652546915966)
XLA Ops:
  0.6 46.8 %shard_map.50 = (f32[64,112]{1,0:T(8,128)}, bf16[8,4,12,8,128]{4,3,2,1,0:T(8,128)(2,1)}) custom-call(f32[2,3,32,8,256]{4,3,2,1,0:T(8,128)} %bitcast.7, f32[3,2,9,8,256]{4,3,2,1,0:T(8,128)} %bitcast.8, bf16[448,6,8,256]{3,2,1,0:T(8,128)(2,1)} %bitcast.6), custom_call_target="tpu_custom_call" | custom-call | tf_op jit(solution)/shard_map/pallas_call | solution.py:531
  47.5 3.5 %shard_map.51 = (f32[64,112]{1,0:T(8,128)}, bf16[8,32,8,192]{3,2,1,0:T(8,128)(2,1)}) custom-call(f32[64,112]{1,0:T(8,128)} %get-tuple-element.6.corr_ref, bf16[8,4,12,8,128]{4,3,2,1,0:T(8,128)(2,1)} %get-tuple-element.7.got_ref), custom_call_target="tpu_custom_call" | custom-call | tf_op jit(solution)/shard_map/pallas_call | solution.py:575

commit v2 on v1

--- a/solution.py
+++ b/solution.py
@@ -23,10 +23,12 @@
 PER_BATCH = NVEC // BATCHES
 HALO_ROWS = PC * PER_BATCH * HALVES
 APPLICATIONS = 4
-STORE_BLOCK = 32
+STORE_BLOCK = 28
 EARLY_BATCHES = 2
 LEADS = (0, 0, 3, 6)
-UNROLL = 2
+STEPS = tuple(
+    sorted(((dx, dz) for dx in range(4) for dz in range(4)), key=lambda d: (-sum(min(a, 4 - a) for a in d), d))
+)
 
 
 def lane_index():
@@ -120,8 +122,10 @@
         return carry
 
     lax.fori_loop(0, PC * NVEC * HALVES // LAYERS, clear, 0)
-    group = lax.broadcasted_iota(jnp.int32, (896, LANES), 0) // LAYERS
-    ones[...] = jnp.where(group == lax.broadcasted_iota(jnp.int32, (896, LANES), 1), 1.0, 0.0).astype(BF16)
+    column = lax.broadcasted_iota(jnp.int32, (1024, LANES), 0)
+    group = jnp.where(column % 256 < STORE_BLOCK * LAYERS, column // 256 * STORE_BLOCK + column % 256 // LAYERS, -1)
+    ones[...] = jnp.where(group == lax.broadcasted_iota(jnp.int32, (1024, LANES), 1), 1.0, 0.0).astype(BF16)
+    diagonal[...] = jnp.zeros_like(diagonal)
     for i in range(5):
         raw_rows[pl.ds(min(i * LAYERS, 28) * ROWS + BELOW, LAYERS, stride=ROWS), :] = zeros
 
@@ -306,7 +310,7 @@
                 apply_pair(level, src, dst, batch * PER_BATCH + 2 * (i // HALVES), lax.rem(i, HALVES))
                 return inner
 
-            lax.fori_loop(0, PER_BATCH, pair, 0, unroll=UNROLL)
+            lax.fori_loop(0, PER_BATCH, pair, 0, unroll=PER_BATCH)
             return carry
 
         lax.fori_loop(first, last, step, 0)
@@ -350,10 +354,16 @@
     own_copy = pltpu.make_async_copy(blocks.at[me_t], got_ref.at[local_t, me_s], own_sem)
 
     def destination(half, i):
-        return half * 16 + lax.rem(x_at + i // 4, 4) * 4 + lax.rem(z_at + i, 4)
+        dx, dz = STEPS[i]
+        return half * 16 + lax.rem(x_at + dx, 4) * 4 + lax.rem(z_at + dz, 4)
 
     def foreign(tm_of):
         return jnp.logical_not(jnp.logical_and(has_self, tm_of == me_t))
+
+    def send_block(tm_of):
+        @pl.when(foreign(tm_of))
+        def _():
+            block_copy(tm_of).start()
 
     def last_half(half):
         def step(batch, carry):
@@ -364,7 +374,7 @@
                 apply_pair(3, a_buf, b_buf, batch * PER_BATCH + 2 * i, half)
                 return inner
 
-            lax.fori_loop(0, PER_BATCH // 2, pair, 0, unroll=UNROLL)
+            lax.fori_loop(0, PER_BATCH // 2, pair, 0, unroll=PER_BATCH // 2)
             return carry
 
         lax.fori_loop(0, BATCHES, step, 0)
@@ -406,16 +416,8 @@
         if half == 0:
             pl.semaphore_wait(met_sem.at[2], len(rings[2]))
 
-        def send_block(i, carry):
-            tm_of = destination(half, i)
-
-            @pl.when(foreign(tm_of))
-            def _():
-                block_copy(tm_of).start()
-
-            return carry
-
-        lax.fori_loop(0, 16, send_block, 0)
+        for i in range(16):
+            send_block(destination(half, i))
 
     last_half(0)
     last_half(1)
@@ -426,25 +428,10 @@
 
     stored_copy.wait()
 
-    def correlate(block, carry):
-        first = pl.multiple_of(block * STORE_BLOCK, STORE_BLOCK)
-        some = [stored[pl.ds(first, STORE_BLOCK), rc].reshape(STORE_BLOCK * LAYERS, 256) for rc in range(PC)]
-        product[...] = lax.dot_general(
-            turned[...], jnp.concatenate(some, axis=1), (((1,), (1,)), ((), ())), preferred_element_type=F32
-        )
-        layer = lax.broadcasted_iota(jnp.int32, (64, STORE_BLOCK * LAYERS), 1) % LAYERS
-        total = product[0:64]
-        for x in range(1, LAYERS):
-            total = jnp.where(layer == x, product[x * 64:(x + 1) * 64], total)
-        diagonal[:, pl.ds(pl.multiple_of(block * 256, 256), 256)] = total
-        return carry
-
-    lax.fori_loop(0, 448 // STORE_BLOCK, correlate, 0)
-
     def part_copy(step):
         other = lax.rem(me_s + step, 4)
         return pltpu.make_async_remote_copy(
-            part_send.at[other],
+            part_send.at[step - 1],
             part_recv.at[step - 1],
             part_send_sem.at[step - 1],
             part_recv_sem.at[step - 1],
@@ -452,15 +439,34 @@
             device_id_type=pl.DeviceIdType.MESH,
         )
 
-    for owner in range(4):
-        values = diagonal[:, owner * 896:(owner + 1) * 896]
+    def correlate(owner):
+        def block(j, carry):
+            first = owner * 112 + j * STORE_BLOCK
+            some = [stored[pl.ds(first, STORE_BLOCK), rc].reshape(STORE_BLOCK * LAYERS, 256) for rc in range(PC)]
+            product[...] = lax.dot_general(
+                turned[...], jnp.concatenate(some, axis=1), (((1,), (1,)), ((), ())), preferred_element_type=F32
+            )
+            layer = lax.broadcasted_iota(jnp.int32, (64, STORE_BLOCK * LAYERS), 1) % LAYERS
+            total = product[0:64]
+            for x in range(1, LAYERS):
+                total = jnp.where(layer == x, product[x * 64:(x + 1) * 64], total)
+            diagonal[j, :, :STORE_BLOCK * LAYERS] = total
+            return carry
+
+        lax.fori_loop(0, 4, block, 0)
+        values = jnp.concatenate([diagonal[j] for j in range(4)], axis=1)
         high = values.astype(BF16)
         low = (values - high.astype(F32)).astype(BF16)
         both = jnp.dot(jnp.concatenate([high, low], axis=0), ones[...], preferred_element_type=F32)
-        part_send[owner] = both[:64] + both[64:]
-    for step in range(1, 4):
+        return both[:64] + both[64:]
+
+    def give(step, carry):
+        part_send[step - 1] = correlate(lax.rem(me_s + step, 4))
         part_copy(step).start()
-    total = part_send[me_s]
+        return carry
+
+    lax.fori_loop(1, 4, give, 0)
+    total = correlate(me_s)
     for step in range(1, 4):
         part_copy(step).wait_recv()
         total = total + part_recv[step - 1]
@@ -481,17 +487,14 @@
     def _():
         own_copy.wait()
 
-    def finish_block(i, carry):
-        for half in range(HALVES):
-            tm_of = destination(half, i)
-
-            @pl.when(foreign(tm_of))
-            def _():
-                block_copy(tm_of).wait_send()
-
-        return carry
-
-    lax.fori_loop(0, 16, finish_block, 0)
+    def finish_block(tm_of):
+        @pl.when(foreign(tm_of))
+        def _():
+            block_copy(tm_of).wait_send()
+
+    for half in range(HALVES):
+        for i in range(16):
+            finish_block(destination(half, i))
 
     def take_block(i, carry):
         tm_of = source_first + i // 4
@@ -515,7 +518,7 @@
 
 def unpack(corr_ref, got_ref, corr_out, solver_out):
     corr_out[...] = corr_ref[...]
-    for t in range(2):
+    for t in range(4):
         for s in range(4):
             solver_out[t, s * 8:(s + 1) * 8, :, :LANES] = got_ref[t, s, 0:8]
             rest = got_ref[t, s, 8:12]
@@ -548,10 +551,10 @@
             pltpu.VMEM((32, 12, 8, LANES), BF16),
             pltpu.VMEM((512, 1536), BF16),
             pltpu.VMEM((512, STORE_BLOCK * LAYERS), F32),
-            pltpu.VMEM((64, 448 * LAYERS), F32),
-            pltpu.VMEM((896, LANES), BF16),
+            pltpu.VMEM((4, 64, 256), F32),
+            pltpu.VMEM((1024, LANES), BF16),
             pltpu.VMEM((2, PC, NVEC * HALVES, LANES), F32),
-            pltpu.VMEM((4, 64, LANES), F32),
+            pltpu.VMEM((3, 64, LANES), F32),
             pltpu.VMEM((3, 64, LANES), F32),
             pltpu.SemaphoreType.DMA((4,)),
             pltpu.SemaphoreType.DMA,
@@ -574,18 +577,18 @@
     )
     corr, solver = pl.pallas_call(
         unpack,
-        grid=(4,),
+        grid=(2,),
         out_shape=(
             jax.ShapeDtypeStruct((64, 112), F32),
             jax.ShapeDtypeStruct((8, 32, 8, 192), BF16),
         ),
         in_specs=[
             pl.BlockSpec((64, 112), lambda i: (0, 0)),
-            pl.BlockSpec((2, 4, 12, 8, LANES), lambda i: (i, 0, 0, 0, 0)),
+            pl.BlockSpec((4, 4, 12, 8, LANES), lambda i: (i, 0, 0, 0, 0)),
         ],
         out_specs=(
             pl.BlockSpec((64, 112), lambda i: (0, 0)),
-            pl.BlockSpec((2, 32, 8, 192), lambda i: (i, 0, 0, 0)),
+            pl.BlockSpec((4, 32, 8, 192), lambda i: (i, 0, 0, 0)),
         ),
     )(corr, got)
     return corr.T[None], solver

time: 51.1 us -> 46.3 us (0.906)
  Pallas kernels: 50.3 us -> 45.6 us
    pallas_call x1, Pallas kernels: 46.8 us -> 43.4 us  [shards(): pl.pallas_call(kernel, out_shape=(jax.ShapeDtypeStruct((64, 112), F32), j...]
    pallas_call x1, Pallas kernels: 3.49 us -> 2.12 us  [shards(): pl.pallas_call(unpack, grid=(2,), out_shape=(jax.ShapeDtypeStruct((64, 11...]
where the time goes in v2:
time: 46.3 us; the launch traced here: 46.2 us
  Pallas kernels  45.6 us (98%)
  between operations  0.64 us (1%)
    pallas_call x1, Pallas kernels, shards(): pl.pallas_call(kernel, out_shape=(jax.ShapeDtypeStruct((64, 112), F32), j...  43.4 us
    pallas_call x1, Pallas kernels, shards(): pl.pallas_call(unpack, grid=(2,), out_shape=(jax.ShapeDtypeStruct((64, 11...  2.12 us

profile of v2, /device:TPU:25, one launch (start us, length us, event | category | flops | bytes accessed | tf_op | source)
XLA Modules:
  0.0 46.2 jit_solution(8702358906534457772)
XLA Ops:
  0.6 43.4 %shard_map.50 = (f32[64,112]{1,0:T(8,128)}, bf16[8,4,12,8,128]{4,3,2,1,0:T(8,128)(2,1)}) custom-call(f32[2,3,32,8,256]{4,3,2,1,0:T(8,128)} %bitcast.7, f32[3,2,9,8,256]{4,3,2,1,0:T(8,128)} %bitcast.8, bf16[448,6,8,256]{3,2,1,0:T(8,128)(2,1)} %bitcast.6), custom_call_target="tpu_custom_call" | custom-call | tf_op jit(solution)/shard_map/pallas_call | solution.py:534
  44.1 2.1 %shard_map.51 = (f32[64,112]{1,0:T(8,128)}, bf16[8,32,8,192]{3,2,1,0:T(8,128)(2,1)}) custom-call(f32[64,112]{1,0:T(8,128)} %get-tuple-element.6.corr_ref, bf16[8,4,12,8,128]{4,3,2,1,0:T(8,128)(2,1)} %get-tuple-element.7.got_ref), custom_call_target="tpu_custom_call" | custom-call | tf_op jit(solution)/shard_map/pallas_call | solution.py:578

commit v3 on v2

--- a/solution.py
+++ b/solution.py
@@ -25,7 +25,8 @@
 APPLICATIONS = 4
 STORE_BLOCK = 28
 EARLY_BATCHES = 2
-LEADS = (0, 0, 3, 6)
+LEADS = (0, 0, 4, 8)
+BEFORE_RELEASE = 2
 STEPS = tuple(
     sorted(((dx, dz) for dx in range(4) for dz in range(4)), key=lambda d: (-sum(min(a, 4 - a) for a in d), d))
 )
@@ -365,7 +366,7 @@
         def _():
             block_copy(tm_of).start()
 
-    def last_half(half):
+    def last_pass(half, start, stop):
         def step(batch, carry):
             if half == 0:
                 correct_ahead(3, a_buf, batch)
@@ -377,15 +378,13 @@
             lax.fori_loop(0, PER_BATCH // 2, pair, 0, unroll=PER_BATCH // 2)
             return carry
 
-        lax.fori_loop(0, BATCHES, step, 0)
-
-        if half == 0:
-            def last_corrections(batch, carry):
-                correct(3, None, batch)
-                return carry
-
-            lax.fori_loop(0, BATCHES, last_corrections, 0)
-
+        lax.fori_loop(start, stop, step, 0)
+
+    def last_corrections(batch, carry):
+        correct(3, None, batch)
+        return carry
+
+    def release(half):
         for side in range(2):
             row = FIRST if side else LAST
             for pc in range(PC):
@@ -419,8 +418,12 @@
         for i in range(16):
             send_block(destination(half, i))
 
-    last_half(0)
-    last_half(1)
+    last_pass(0, 0, BATCHES)
+    last_pass(1, 0, BEFORE_RELEASE)
+    lax.fori_loop(0, BATCHES, last_corrections, 0)
+    release(0)
+    last_pass(1, BEFORE_RELEASE, BATCHES)
+    release(1)
 
     @pl.when(has_self)
     def _():

time: 46.3 us -> 45.3 us (0.978)
  Pallas kernels: 45.6 us -> 44.5 us
    pallas_call x1, Pallas kernels: 43.4 us -> 42.3 us  [shards(): pl.pallas_call(kernel, out_shape=(jax.ShapeDtypeStruct((64, 112), F32), j...]
where the time goes in v3:
time: 45.3 us; the launch traced here: 45.1 us
  Pallas kernels  44.5 us (98%)
  between operations  0.64 us (1%)
    pallas_call x1, Pallas kernels, shards(): pl.pallas_call(kernel, out_shape=(jax.ShapeDtypeStruct((64, 112), F32), j...  42.3 us
    pallas_call x1, Pallas kernels, shards(): pl.pallas_call(unpack, grid=(2,), out_shape=(jax.ShapeDtypeStruct((64, 11...  2.12 us

profile of v3, /device:TPU:25, one launch (start us, length us, event | category | flops | bytes accessed | tf_op | source)
XLA Modules:
  0.0 45.1 jit_solution(3736577930778459878)
XLA Ops:
  0.6 42.3 %shard_map.50 = (f32[64,112]{1,0:T(8,128)}, bf16[8,4,12,8,128]{4,3,2,1,0:T(8,128)(2,1)}) custom-call(f32[2,3,32,8,256]{4,3,2,1,0:T(8,128)} %bitcast.7, f32[3,2,9,8,256]{4,3,2,1,0:T(8,128)} %bitcast.8, bf16[448,6,8,256]{3,2,1,0:T(8,128)(2,1)} %bitcast.6), custom_call_target="tpu_custom_call" | custom-call | tf_op jit(solution)/shard_map/pallas_call | solution.py:537
  43.0 2.1 %shard_map.51 = (f32[64,112]{1,0:T(8,128)}, bf16[8,32,8,192]{3,2,1,0:T(8,128)(2,1)}) custom-call(f32[64,112]{1,0:T(8,128)} %get-tuple-element.6.corr_ref, bf16[8,4,12,8,128]{4,3,2,1,0:T(8,128)(2,1)} %get-tuple-element.7.got_ref), custom_call_target="tpu_custom_call" | custom-call | tf_op jit(solution)/shard_map/pallas_call | solution.py:581

commit v4 on v3

--- a/solution.py
+++ b/solution.py
@@ -470,34 +470,35 @@
 
     lax.fori_loop(1, 4, give, 0)
     total = correlate(me_s)
+
+    def finish_halo(i, carry):
+        for level in range(APPLICATIONS):
+            for side in range(2):
+                halo_copy(level, side, i).wait_send()
+        return carry
+
+    lax.fori_loop(0, BATCHES, finish_halo, 0)
+    top_copy.wait_send()
+    for step in range(1, 4):
+        part_copy(step).wait_send()
+
+    @pl.when(has_self)
+    def _():
+        own_copy.wait()
+
+    def finish_block(tm_of):
+        @pl.when(foreign(tm_of))
+        def _():
+            block_copy(tm_of).wait_send()
+
+    for half in range(HALVES):
+        for i in range(16):
+            finish_block(destination(half, i))
+
     for step in range(1, 4):
         part_copy(step).wait_recv()
         total = total + part_recv[step - 1]
     corr_ref[...] = total[:, :112]
-
-    def finish_halo(i, carry):
-        for level in range(APPLICATIONS):
-            for side in range(2):
-                halo_copy(level, side, i).wait_send()
-        return carry
-
-    lax.fori_loop(0, BATCHES, finish_halo, 0)
-    top_copy.wait_send()
-    for step in range(1, 4):
-        part_copy(step).wait_send()
-
-    @pl.when(has_self)
-    def _():
-        own_copy.wait()
-
-    def finish_block(tm_of):
-        @pl.when(foreign(tm_of))
-        def _():
-            block_copy(tm_of).wait_send()
-
-    for half in range(HALVES):
-        for i in range(16):
-            finish_block(destination(half, i))
 
     def take_block(i, carry):
         tm_of = source_first + i // 4

time: 45.3 us -> 45.3 us (level)
  no operation moved by 1% of the time
where the time goes in v4:
time: 45.3 us; the launch traced here: 44.9 us
  Pallas kernels  44.2 us (98%)
  between operations  0.64 us (1%)
    pallas_call x1, Pallas kernels, shards(): pl.pallas_call(kernel, out_shape=(jax.ShapeDtypeStruct((64, 112), F32), j...  42.1 us
    pallas_call x1, Pallas kernels, shards(): pl.pallas_call(unpack, grid=(2,), out_shape=(jax.ShapeDtypeStruct((64, 11...  2.12 us

profile of v4, /device:TPU:25, one launch (start us, length us, event | category | flops | bytes accessed | tf_op | source)
XLA Modules:
  0.0 44.9 jit_solution(6040199952355513903)
XLA Ops:
  0.6 42.1 %shard_map.50 = (f32[64,112]{1,0:T(8,128)}, bf16[8,4,12,8,128]{4,3,2,1,0:T(8,128)(2,1)}) custom-call(f32[2,3,32,8,256]{4,3,2,1,0:T(8,128)} %bitcast.7, f32[3,2,9,8,256]{4,3,2,1,0:T(8,128)} %bitcast.8, bf16[448,6,8,256]{3,2,1,0:T(8,128)(2,1)} %bitcast.6), custom_call_target="tpu_custom_call" | custom-call | tf_op jit(solution)/shard_map/pallas_call | solution.py:538
  42.8 2.1 %shard_map.51 = (f32[64,112]{1,0:T(8,128)}, bf16[8,32,8,192]{3,2,1,0:T(8,128)(2,1)}) custom-call(f32[64,112]{1,0:T(8,128)} %get-tuple-element.6.corr_ref, bf16[8,4,12,8,128]{4,3,2,1,0:T(8,128)(2,1)} %get-tuple-element.7.got_ref), custom_call_target="tpu_custom_call" | custom-call | tf_op jit(solution)/shard_map/pallas_call | solution.py:582
